TPU v7x, 256 devices: a whole 4x4x8 slice. The times are simulated.
256 devices in a mesh: dp: 64 (over y, z_hi, x), tensor: 4 (over z_lo, core).
Axes of the slice: x: 4, y: 4, z: 8 (z_hi: 4, z_lo: 2; z = z_hi * 2 + z_lo), core: 2. Of those that a mesh axis runs over, the one named last changes fastest.
Arguments:
- activations: bfloat16 [32768, 4096], P('dp'), may hold values from -1000 to 1000
- norm_gain: bfloat16 [4096], replicated, may hold values from 0.5 to 1.5
- query_blocks: bfloat16 [128, 32, 4096], P('dp', None, 'tensor'), may hold values from -64 to 64
- query_scales: int32 [128, 1, 4096], P('dp', None, 'tensor'), may hold values from -9 to -5
- key_blocks: bfloat16 [128, 32, 512], P('dp', None, 'tensor'), may hold values from -64 to 64
- key_scales: int32 [128, 1, 512], P('dp', None, 'tensor'), may hold values from -9 to -5
- value_blocks: bfloat16 [128, 32, 512], P('dp', None, 'tensor'), may hold values from -6 to 6
- value_scales: int32 [128, 1, 512], P('dp', None, 'tensor'), may hold values from -9 to -5
- output_blocks: bfloat16 [128, 32, 4096], P('tensor', None, 'dp'), may hold values from -6 to 6
- output_scales: int32 [128, 1, 4096], P('tensor', None, 'dp'), may hold values from -9 to -5
Outputs:
- attended: bfloat16 [32768, 4096], P('dp')
All inputs are finite; a program needn't handle non-finite values.
Results may differ from a plain program's by a relative error of at most 0.015.
The roundings to bfloat16 on the way count: a program that leaves them out, or rounds other values in their place, can miss the bound.
Values may be sent and summed in bfloat16 or wider, within the bound.
A program may use at most 128 MiB of HBM per device.

v0:
```python
import math
import jax
import jax.numpy as jnp
from jax import lax
from jax.sharding import PartitionSpec as P

HEAD_DIM = 128
SEQ = 256
EPS = 1e-05
ROPE_BASE = 500000.0


def turned_gather(arrays, axis, dims):
    turned = [jnp.moveaxis(a, dim, 0) for a, dim in zip(arrays, dims)]
    widths = [t[0].size for t in turned]
    both = jnp.concatenate([t.reshape(-1, w) for t, w in zip(turned, widths)], axis=1)
    out = lax.all_gather(both, axis, axis=0, tiled=True)
    blocks = jnp.split(out, [sum(widths[:k]) for k in range(1, len(widths))], axis=1)
    return tuple(
        (
            jnp.moveaxis(b.reshape(-1, *t.shape[1:]), 0, dim)
            for b, t, dim in zip(blocks, turned, dims)
        )
    )


def side_by_side(arrays, axis, dim, along):
    widths = [math.prod(a.shape[along:]) for a in arrays]
    both = jnp.concatenate(
        [a.reshape(*a.shape[:along], w) for a, w in zip(arrays, widths)], axis=along
    )
    out = lax.all_gather(both, axis, axis=dim, tiled=True)
    blocks = jnp.split(out, [sum(widths[:k]) for k in range(1, len(widths))], axis=along)
    return tuple((b.reshape(*out.shape[:along], *a.shape[along:]) for a, b in zip(arrays, blocks)))


def dequant(blocks, scales):
    factor = jnp.exp2(scales.astype(jnp.float32)).astype(blocks.dtype)
    weight = blocks * factor
    return weight.reshape(weight.shape[0] * weight.shape[1], weight.shape[2])


def rotate_pairs(states, positions):
    half_dim = states.shape[-1] // 2
    frequency = jnp.exp(
        -math.log(ROPE_BASE) * jnp.arange(half_dim, dtype=jnp.float32) * 2.0 / states.shape[-1]
    )
    angles = positions.astype(jnp.float32)[:, None] * frequency[None, :]
    cosine = jnp.cos(angles)[None, :, None, :]
    sine_part = jnp.sin(angles)[None, :, None, :]
    first = states[..., :half_dim]
    second = states[..., half_dim:]
    return jnp.concatenate(
        [first * cosine - second * sine_part, second * cosine + first * sine_part], axis=-1
    )


def attend(query_states, key_states, value_states, kv_count):
    tokens_here = query_states.shape[0]
    count = tokens_here // SEQ
    positions = jnp.arange(SEQ, dtype=jnp.int32)
    queries = rotate_pairs(query_states.reshape(count, SEQ, -1, HEAD_DIM), positions).astype(
        jnp.bfloat16
    )
    rotated_keys = rotate_pairs(
        key_states.reshape(count, SEQ, kv_count, HEAD_DIM), positions
    ).astype(jnp.bfloat16)
    value_heads = value_states.astype(jnp.bfloat16).reshape(count, SEQ, kv_count, HEAD_DIM)
    group_size = queries.shape[2] // kv_count
    queries = queries.reshape(count, SEQ, kv_count, group_size, HEAD_DIM)
    scores = jnp.einsum(
        "sqkgd,stkd->skgqt", queries, rotated_keys, preferred_element_type=jnp.float32
    ) * HEAD_DIM ** (-0.5)
    visible = positions[:, None] >= positions[None, :]
    scores = jnp.where(visible, scores, -jnp.inf)
    attn_weights = jax.nn.softmax(scores, axis=-1).astype(jnp.bfloat16)
    context = jnp.einsum(
        "skgqt,stkd->sqkgd", attn_weights, value_heads, preferred_element_type=jnp.float32
    )
    return context.astype(jnp.bfloat16).reshape(tokens_here, -1)


def shards(
    activations,
    norm_gain,
    query_blocks,
    query_scales,
    key_blocks,
    key_scales,
    value_blocks,
    value_scales,
    output_blocks,
    output_scales,
):
    query_exps = query_scales.astype(jnp.bfloat16)
    key_exps = key_scales.astype(jnp.bfloat16)
    value_exps = value_scales.astype(jnp.bfloat16)
    output_exps = output_scales.astype(jnp.bfloat16)
    output_whole = turned_gather((output_blocks, output_exps), "dp", (2, 2))
    wide_rows = activations.astype(jnp.float32)
    inverse = lax.rsqrt(jnp.mean(wide_rows * wide_rows, axis=-1, keepdims=True) + EPS)
    normed = (wide_rows * inverse * norm_gain.astype(jnp.float32)).astype(jnp.bfloat16)

    def product(blocks, scales):
        return jnp.dot(normed, dequant(blocks, scales), preferred_element_type=jnp.float32)

    pieces = side_by_side(
        (query_blocks, query_exps, key_blocks, key_exps, value_blocks, value_exps), "dp", 0, 1
    )
    query_states = product(pieces[0], pieces[1])
    key_states = product(pieces[2], pieces[3])
    value_states = product(pieces[4], pieces[5])
    context = attend(query_states, key_states, value_states, key_blocks.shape[2] // HEAD_DIM)
    partial_value = jnp.dot(
        context, dequant(output_whole[0], output_whole[1]), preferred_element_type=jnp.float32
    )
    return lax.psum(partial_value.astype(jnp.bfloat16), "tensor")


def solution(mesh):
    placed = (
        P("dp", None),
        P(),
        P("dp", None, "tensor"),
        P("dp", None, "tensor"),
        P("dp", None, "tensor"),
        P("dp", None, "tensor"),
        P("dp", None, "tensor"),
        P("dp", None, "tensor"),
        P("tensor", None, "dp"),
        P("tensor", None, "dp"),
    )
    return jax.shard_map(
        shards, mesh=mesh, in_specs=placed, out_specs=P("dp", None), check_vma=False
    )
```

profile of v0, /device:TPU:1, one launch (start us, length us, event | category | flops | bytes accessed | tf_op | source)
XLA Modules:
  0.0 459.1 jit_solution(9904622550752400796)
XLA Ops:
  6.5 0.7 convert_bitcast_fusion
  7.3 1.0 pad_maximum_fusion
  8.3 0.8 copy.48
  9.1 0.0 all-gather.4.cloned.1.call-update
  9.1 0.0 all-gather.6.cloned.1.call-start
  9.2 1.0 copy.64
  10.2 0.1 constant_dynamic-update-slice_fusion.3
  10.3 0.7 constant_dynamic-update-slice_fusion.2
  11.0 0.7 bitcast_dynamic-update-slice_fusion.1
  11.8 0.7 constant_dynamic-update-slice_fusion.1
  12.4 0.7 bitcast_dynamic-update-slice_fusion
  13.2 0.7 constant_dynamic-update-slice_fusion
  13.9 0.7 copy-done.2
  14.6 0.0 all-reduce.2.cloned.1.call-start
  14.6 0.9 convert_element_type.104
  15.5 3.3 fusion
  18.9 0.3 multiply_cosine_fusion
  19.2 3.6 fusion.2
  22.8 106.9 %all-gather.4.cloned.1.call-done = bf16[4096,1056]{1,0:T(8,128)(2,1)} async-done(((bf16[64,1056]{1,0:T(8,128)(2,1)}), bf16[4096,1056]{1,0:T(8,128)(2,1)}) %all-gather.4.cloned.1.call-update) | async-done | bytes 8650768 | tf_op jit(solution)/shard_map/all_gather | solution.py:17
  129.7 1.6 fusion.14
  131.3 0.3 copy.50
  131.6 7.7 %split.38 = bf16[4096,1024]{1,0:T(8,128)(2,1)} slice(bf16[4096,1056]{1,0:T(8,128)(2,1)} %all-gather.4.cloned.1.call-done), slice={[0:4096], [0:1024]} | slice | bytes 16777216 | tf_op jit(solution)/shard_map/split | solution.py:18
  139.3 11.4 %copy.63 = bf16[4096,1024]{0,1:T(8,128)(2,1)} copy(bf16[4096,1024]{1,0:T(8,128)(2,1)} %split.38) | data formatting | bytes 16777216
  150.7 7.4 %broadcast_multiply_fusion = bf16[32,32,4096]{2,1,0:T(8,128)(2,1)} fusion(bf16[32,32,4096]{2,1,0:T(8,128)(2,1)} %bitcast.115, bf16[32,4096]{1,0:T(8,128)(2,1)S(1)} %copy.50), kind=kLoop, calls=%fused_computation.8 | loop fusion | flops 4194304 | bytes 17039360 | tf_op jit(solution)/shard_map/mul | solution.py:39
  158.1 97.6 %all-gather.6.cloned.1.call-done = bf16[64,2,42240]{2,1,0:T(2,128)(2,1)} async-done(((bf16[1,2,42240]{2,1,0:T(2,128)(2,1)}), bf16[64,2,42240]{2,1,0:T(2,128)(2,1)}) %all-gather.6.cloned.1.call-update) | async-done | bytes 10813456 | tf_op jit(solution)/shard_map/all_gather | solution.py:32
  255.7 14.6 %reshape.197 = bf16[128,42240]{1,0:T(8,128)(2,1)} reshape(bf16[64,2,42240]{2,1,0:T(2,128)(2,1)} %all-gather.6.cloned.1.call-done) | data formatting | bytes 21626880
  270.4 0.8 exponential_convert_fusion.2
  271.2 1.0 exponential_convert_fusion.1
  272.2 7.3 %split.36 = bf16[128,32768]{1,0:T(8,128)(2,1)} slice(bf16[128,42240]{1,0:T(8,128)(2,1)} %reshape.197), slice={[0:128], [0:32768]} | slice | bytes 16777216 | tf_op jit(solution)/shard_map/split | solution.py:33
  279.5 0.1 mul.220
  279.7 1.9 bitcast_multiply_fusion.1
  281.6 13.5 %reshape.189 = bf16[4096,1024]{1,0:T(8,128)(2,1)} reshape(bf16[128,32768]{1,0:T(8,128)(2,1)} %split.36) | data formatting | bytes 16777216 | tf_op jit(solution)/shard_map/reshape | solution.py:34
  295.1 7.2 %bitcast_multiply_fusion = bf16[4096,1024]{1,0:T(8,128)(2,1)} fusion(bf16[4096,1024]{1,0:T(8,128)(2,1)} %reshape.189, bf16[128,1024]{1,0:T(8,128)(2,1)S(1)} %exponential_convert_fusion.1), kind=kLoop, calls=%fused_computation.5 | loop fusion | flops 4194304 | bytes 17039360 | tf_op jit(solution)/shard_map/mul | solution.py:39
  302.3 11.4 %copy.62 = bf16[1024,4096]{1,0:T(8,128)(2,1)} copy(bf16[1024,4096]{0,1:T(8,128)(2,1)} %bitcast.116) | data formatting | bytes 16777216 | tf_op jit(solution)/shard_map/dot_general | solution.py:105
  313.7 0.5 mul.223
  314.3 0.5 reshape.187
  314.8 0.1 bitcast_multiply_fusion.2
  314.9 3.6 convolution_convert_fusion.1
  318.5 7.4 %fusion.30 = f32[2,256,8,128]{1,3,2,0:T(8,128)S(1)} fusion(bf16[2,256,4096,1]{2,1,3,0:T(8,128)(2,1)S(1)} %bitcast.117, bf16[8,128,4096,1]{2,1,0,3:T(8,128)(2,1)} %bitcast.120), kind=kOutput, calls=%fused_computation.62 | convolution fusion | flops 4294967296 | bytes 14680064 | tf_op jit(solution)/shard_map/dot_general | solution.py:105
  325.9 1.5 convolution_bitcast_fusion
  327.4 0.3 subtract_convert_fusion
  327.8 0.8 fusion.4
  328.6 0.9 fusion.3
  329.5 1.3 fusion.11
  330.8 0.8 copy.46
  331.6 9.4 %convolution_convert_fusion = bf16[512,4096]{1,0:T(8,128)(2,1)} fusion(bf16[1024,4096]{1,0:T(8,128)(2,1)} %bitcast.119, bf16[64,8,8,128]{3,2,1,0:T(8,128)(2,1)S(1)} %bitcast.122), kind=kOutput, calls=%fused_computation.6 | convolution fusion | flops 4297064448 | bytes 13631488 | tf_op jit(solution)/shard_map/dot_general | solution.py:114
  341.0 106.9 %all-reduce.2.cloned.1.call-done = bf16[512,4096]{1,0:T(8,128)(2,1)} async-done(((bf16[512,4096]{1,0:T(8,128)(2,1)}), bf16[512,4096]{1,0:T(8,128)(2,1)}) %all-reduce.2.cloned.1.call-update) | async-done | bytes 4194320 | tf_op jit(solution)/shard_map/psum | solution.py:117
  447.9 4.7 %copy.87 = bf16[512,4096]{1,0:T(8,128)(2,1)} copy(bf16[512,4096]{1,0:T(8,128)(2,1)} %all-reduce.2.cloned.1.call-done) | data formatting | bytes 8388608
  (13 shorter events, 0.1 us)
Async XLA Ops:
  6.5 123.2 %all-gather.4.cloned.1.call-start = ((), (), s32[]{:S(2)}) async-start(), calls=%async_computation | async-start | bytes 9584640 | tf_op jit(solution)/shard_map/all_gather | solution.py:17
  9.1 246.6 %all-gather.6.cloned.1.call-start = ((), (), s32[]{:S(2)}) async-start(), calls=%async_computation.2 | async-start | bytes 10982400 | tf_op jit(solution)/shard_map/all_gather | solution.py:32
  13.9 0.7 copy-start.2
  14.6 433.3 %all-reduce.2.cloned.1.call-start = ((), (), s32[]{:S(2)}) async-start(), calls=%async_computation.1 | async-start | bytes 8388608 | tf_op jit(solution)/shard_map/psum | solution.py:117
  14.6 4.5 copy-start
  314.8 3.7 copy-start.1
Sparse Core Ops, SparseCore 0:
  10.5 119.1 all-gather.3
  133.0 122.6 all-gather.5
  341.1 106.7 all-reduce.1
where the time goes:
time: 461 us; the launch traced here: 459 us
  waiting for transfers between devices  311 us (67%)
  local copies, waits for them, and re-layouts  77 us (17%)
  other arithmetic  33.3 us (7%)
  matrix products  24 us (5%)
  between operations  13.3 us (3%)
    all_gather x1, waiting for transfers between devices, turned_gather(): out = lax.all_gather(both, axis, axis=0, tiled=True)  107 us
    psum x1, waiting for transfers between devices, shards(): return lax.psum(partial_value.astype(jnp.bfloat16), 'tensor')  107 us
    all_gather x1, waiting for transfers between devices, side_by_side(): out = lax.all_gather(both, axis, axis=dim, tiled=True)  97.6 us
    unnamed x13, local copies, waits for them, and re-layouts  34 us
    mul x5, other arithmetic, dequant(): weight = blocks * factor  18.2 us
    reshape x2, local copies, waits for them, and re-layouts, side_by_side(): b.reshape(*out.shape[:along], *a.shape[along:])  14 us
    dot_general x3, matrix products, product(): jnp.dot(normed, dequant(blocks, scales), preferred_element_type=jnp.float32)  12.5 us
    dot_general x1, local copies, waits for them, and re-layouts, product(): jnp.dot(normed, dequant(blocks, scales), preferred_element_type=jnp.float32)  11.4 us
  transfers between devices with their start and end apart: 3, of which 3 were waited for; matrix products, arithmetic and copies ran while one was open for 9% of the time, Pallas kernels for 0%

commit v1 on v0

--- a/solution.py
+++ b/solution.py
@@ -14,7 +14,9 @@
     turned = [jnp.moveaxis(a, dim, 0) for a, dim in zip(arrays, dims)]
     widths = [t[0].size for t in turned]
     both = jnp.concatenate([t.reshape(-1, w) for t, w in zip(turned, widths)], axis=1)
-    out = lax.all_gather(both, axis, axis=0, tiled=True)
+    out = jnp.concatenate(
+        lax.all_to_all(jnp.stack([both] * lax.axis_size(axis)), axis, 0, 0), axis=0
+    )
     blocks = jnp.split(out, [sum(widths[:k]) for k in range(1, len(widths))], axis=1)
     return tuple(
         (

time: 461 us -> 542 us (1.18)
  waiting for transfers between devices: 311 us -> 373 us
  starting transfers between devices: 0.09 us -> 15.5 us
    all_to_all x0 -> x1, waiting for transfers between devices: none -> 265 us  [turned_gather(): lax.all_to_all(jnp.stack([both] * lax.axis_size(axis)), axis, 0, 0)]
    all_gather x1 -> x0, waiting for transfers between devices: 107 us -> none  [turned_gather(): out = lax.all_gather(both, axis, axis=0, tiled=True)]
    all_gather x1, waiting for transfers between devices: 97.6 us -> 0.01 us  [side_by_side(): out = lax.all_gather(both, axis, axis=dim, tiled=True)]
    all_to_all x0 -> x1, starting transfers between devices: none -> 15.5 us  [turned_gather(): lax.all_to_all(jnp.stack([both] * lax.axis_size(axis)), axis, 0, 0)]
    split x1 -> x2, local copies, waits for them, and re-layouts: 7.67 us -> 19.2 us  [turned_gather(): jnp.split(out, [sum(widths[:k]) for k in range(1, len(widths))], axis=1)]
    unnamed x13 -> x14, local copies, waits for them, and re-layouts: 34 us -> 22.7 us
  transfers between devices with their start and end apart: 3 -> 3, of which waited for: 3 -> 2; matrix products, arithmetic and copies ran while one was open for 9% -> 8% of each run, Pallas kernels for 0% -> 0%
where the time goes in v1:
time: 542 us; the launch traced here: 540 us
  waiting for transfers between devices  373 us (69%)
  local copies, waits for them, and re-layouts  81.5 us (15%)
  other arithmetic  32.3 us (6%)
  matrix products  24 us (4%)
  starting transfers between devices  15.5 us (3%)
  between operations  13.6 us (3%)
    all_to_all x1, waiting for transfers between devices, turned_gather(): lax.all_to_all(jnp.stack([both] * lax.axis_size(axis)), axis, 0, 0)  265 us
    psum x1, waiting for transfers between devices, shards(): return lax.psum(partial_value.astype(jnp.bfloat16), 'tensor')  108 us
    unnamed x14, local copies, waits for them, and re-layouts  22.7 us
    split x2, local copies, waits for them, and re-layouts, turned_gather(): jnp.split(out, [sum(widths[:k]) for k in range(1, len(widths))], axis=1)  19.2 us
    mul x5, other arithmetic, dequant(): weight = blocks * factor  18.1 us
    all_to_all x1, starting transfers between devices, turned_gather(): lax.all_to_all(jnp.stack([both] * lax.axis_size(axis)), axis, 0, 0)  15.5 us
    reshape x2, local copies, waits for them, and re-layouts, side_by_side(): b.reshape(*out.shape[:along], *a.shape[along:])  14 us
    dot_general x3, matrix products, product(): jnp.dot(normed, dequant(blocks, scales), preferred_element_type=jnp.float32)  12.5 us
  transfers between devices with their start and end apart: 3, of which 2 were waited for; matrix products, arithmetic and copies ran while one was open for 8% of the time, Pallas kernels for 0%

profile of v1, /device:TPU:1, one launch (start us, length us, event | category | flops | bytes accessed | tf_op | source)
XLA Modules:
  0.0 540.1 jit_solution(4302217105830840284)
XLA Ops:
  6.5 1.0 copy.62
  7.6 0.1 constant_dynamic-update-slice_fusion.3
  7.7 0.7 constant_dynamic-update-slice_fusion.2
  8.4 0.7 bitcast_dynamic-update-slice_fusion.1
  9.1 0.7 constant_dynamic-update-slice_fusion.1
  9.8 0.7 bitcast_dynamic-update-slice_fusion
  10.6 0.7 constant_dynamic-update-slice_fusion
  11.2 0.7 copy-done.2
  11.9 0.0 all-gather.3.cloned.1.call-update
  12.0 0.7 convert_bitcast_fusion
  12.7 1.0 pad_maximum_fusion
  13.7 0.2 copy.47
  13.9 4.9 stack.2
  18.8 15.5 %all-to-all-start = ((bf16[64,64,1056]{2,1,0:T(8,128)(2,1)}), bf16[64,64,1056]{2,1,0:T(8,128)(2,1)}, u32[]{:S(2)}, u32[]{:S(2)}) async-start(bf16[64,64,1056]{2,1,0:T(8,128)(2,1)} %stack.2), calls=%async_computation | async-start | bytes 18874368 | tf_op jit(solution)/shard_map/all_to_all | solution.py:18
  34.2 0.0 all-reduce.2.cloned.1.call-start
  34.4 3.3 fusion
  37.7 0.3 multiply_cosine_fusion
  38.0 3.6 fusion.2
  41.6 265.4 %all-to-all-done = bf16[64,64,1056]{2,1,0:T(8,128)(2,1)} async-done(((bf16[64,64,1056]{2,1,0:T(8,128)(2,1)}), bf16[64,64,1056]{2,1,0:T(8,128)(2,1)}, u32[]{:S(2)}, u32[]{:S(2)}) %all-to-all-start) | async-done | bytes 8650784 | tf_op jit(solution)/shard_map/all_to_all | solution.py:18
  307.1 7.7 %split.38 = bf16[4096,1024]{1,0:T(8,128)(2,1)} slice(bf16[4096,1056]{1,0:T(8,128)(2,1)} %bitcast.31), slice={[0:4096], [0:1024]} | slice | bytes 16777216 | tf_op jit(solution)/shard_map/split | solution.py:20
  314.8 1.6 fusion.14
  316.3 0.3 copy.49
  316.6 11.6 %copy.48 = bf16[4096,1024]{0,1:T(8,128)(2,1)} copy(bf16[4096,1024]{1,0:T(8,128)(2,1)} %split.38) | data formatting | bytes 16777216 | tf_op jit(solution)/shard_map/split | solution.py:20
  328.2 7.3 %broadcast_multiply_fusion = bf16[32,32,4096]{2,1,0:T(8,128)(2,1)} fusion(bf16[32,32,4096]{2,1,0:T(8,128)(2,1)} %bitcast.116, bf16[32,4096]{1,0:T(8,128)(2,1)S(1)} %copy.49), kind=kLoop, calls=%fused_computation.8 | loop fusion | flops 4194304 | bytes 17039360 | tf_op jit(solution)/shard_map/mul | solution.py:41
  335.6 14.6 %reshape.203 = bf16[128,42240]{1,0:T(8,128)(2,1)} reshape(bf16[64,2,42240]{2,1,0:T(2,128)(2,1)} %all-gather.3.cloned.1.call-done) | data formatting | bytes 21626880
  350.2 0.8 exponential_convert_fusion.2
  351.0 1.0 exponential_convert_fusion.1
  352.1 7.3 %split.36 = bf16[128,32768]{1,0:T(8,128)(2,1)} slice(bf16[128,42240]{1,0:T(8,128)(2,1)} %reshape.203), slice={[0:128], [0:32768]} | slice | bytes 16777216 | tf_op jit(solution)/shard_map/split | solution.py:35
  359.4 0.1 mul.220
  359.5 1.9 bitcast_multiply_fusion.1
  361.5 13.5 %reshape.194 = bf16[4096,1024]{1,0:T(8,128)(2,1)} reshape(bf16[128,32768]{1,0:T(8,128)(2,1)} %split.36) | data formatting | bytes 16777216 | tf_op jit(solution)/shard_map/reshape | solution.py:36
  375.0 7.2 %bitcast_multiply_fusion = bf16[4096,1024]{1,0:T(8,128)(2,1)} fusion(bf16[4096,1024]{1,0:T(8,128)(2,1)} %reshape.194, bf16[128,1024]{1,0:T(8,128)(2,1)S(1)} %exponential_convert_fusion.1), kind=kLoop, calls=%fused_computation.5 | loop fusion | flops 4194304 | bytes 17039360 | tf_op jit(solution)/shard_map/mul | solution.py:41
  382.2 11.4 %copy.61 = bf16[1024,4096]{1,0:T(8,128)(2,1)} copy(bf16[1024,4096]{0,1:T(8,128)(2,1)} %bitcast.117) | data formatting | bytes 16777216 | tf_op jit(solution)/shard_map/dot_general | solution.py:107
  393.6 0.5 mul.223
  394.1 0.5 reshape.192
  394.7 0.1 bitcast_multiply_fusion.2
  394.8 3.6 convolution_convert_fusion.1
  398.4 7.4 %fusion.30 = f32[2,256,8,128]{1,3,2,0:T(8,128)S(1)} fusion(bf16[2,256,4096,1]{2,1,3,0:T(8,128)(2,1)S(1)} %bitcast.118, bf16[8,128,4096,1]{2,1,0,3:T(8,128)(2,1)} %bitcast.121), kind=kOutput, calls=%fused_computation.62 | convolution fusion | flops 4294967296 | bytes 14680064 | tf_op jit(solution)/shard_map/dot_general | solution.py:107
  405.7 1.5 convolution_bitcast_fusion
  407.3 0.3 subtract_convert_fusion
  407.7 0.8 fusion.4
  408.5 0.9 fusion.3
  409.4 1.3 fusion.11
  410.7 0.8 copy.45
  411.4 9.4 %convolution_convert_fusion = bf16[512,4096]{1,0:T(8,128)(2,1)} fusion(bf16[1024,4096]{1,0:T(8,128)(2,1)} %bitcast.120, bf16[64,8,8,128]{3,2,1,0:T(8,128)(2,1)S(1)} %bitcast.123), kind=kOutput, calls=%fused_computation.6 | convolution fusion | flops 4297064448 | bytes 13631488 | tf_op jit(solution)/shard_map/dot_general | solution.py:116
  420.8 0.0 all-reduce.2.cloned.1.call-update
  420.9 107.7 %all-reduce.2.cloned.1.call-done = bf16[512,4096]{1,0:T(8,128)(2,1)} async-done(((bf16[512,4096]{1,0:T(8,128)(2,1)}), bf16[512,4096]{1,0:T(8,128)(2,1)}) %all-reduce.2.cloned.1.call-update) | async-done | bytes 4194320 | tf_op jit(solution)/shard_map/psum | solution.py:119
  528.5 4.7 copy.85
  (15 shorter events, 0.1 us)
Async XLA Ops:
  6.5 329.0 %all-gather.3.cloned.1.call-start = ((), (), s32[]{:S(2)}) async-start(), calls=%async_computation.2 | async-start | bytes 10982400 | tf_op jit(solution)/shard_map/all_gather | solution.py:34
  11.2 0.7 copy-start.2
  18.8 15.5 %copy-start.3 = (bf16[4096]{0:T(1024)(128)(2,1)S(1)}, bf16[4096]{0:T(1024)(128)(2,1)}, u32[]{:S(2)}) copy-start(bf16[4096]{0:T(1024)(128)(2,1)} %param.11) | copy-start | bytes 24580
  18.8 288.3 %all-to-all-start = ((bf16[64,64,1056]{2,1,0:T(8,128)(2,1)}), bf16[64,64,1056]{2,1,0:T(8,128)(2,1)}, u32[]{:S(2)}, u32[]{:S(2)}) async-start(bf16[64,64,1056]{2,1,0:T(8,128)(2,1)} %stack.2), calls=%async_computation | async-start | bytes 18874368 | tf_op jit(solution)/shard_map/all_to_all | solution.py:18
  34.2 494.3 %all-reduce.2.cloned.1.call-start = ((), (), s32[]{:S(2)}) async-start(), calls=%async_computation.1 | async-start | bytes 8388608 | tf_op jit(solution)/shard_map/psum | solution.py:119
  34.3 3.7 copy-start
  394.7 3.7 copy-start.1
Sparse Core Ops, SparseCore 0:
  12.1 298.6 all-gather.2
  421.0 107.4 all-reduce.1
